TPU v7x, 128 devices: a whole 4x4x4 slice. The times are simulated.
128 devices in a mesh: enc: 32 (over z, x, core), llm: 4 (over y).
Axes of the slice: x: 4, y: 4, z: 4, core: 2. Of those that a mesh axis runs over, the one named last changes fastest.
Arguments:
- patches: bfloat16 [16384, 5120], P('enc', 'llm'), may hold values from -6 to 6
- ln_gain: bfloat16 [1280], replicated, may hold values from 0.099609375 to 1.8984375
- w_in: bfloat16 [5120, 5120], P(None, 'llm'), may hold values from -0.078125 to 0.078125
- b_in: bfloat16 [5120], P('llm'), may hold values from -3 to 3
- w_out: bfloat16 [5120, 2048], P('llm'), may hold values from -0.078125 to 0.078125
- b_out: bfloat16 [2048], replicated, may hold values from -3 to 3
- owner: int32 [16384, 1], P(('enc', 'llm')), may hold values from 0 to 127; in each aligned block of 128 rows (0 to 127, 128 to 255, ...) at most 2 rows name the same one
- cotangent: bfloat16 [32768, 2048], P(('enc', 'llm')), may hold values from -6 to 6
Outputs:
- image_embeds: bfloat16 [32768, 2048], P(('enc', 'llm'))
- grad_w_in: float32 [5120, 5120], P('enc', 'llm')
- grad_w_out: float32 [5120, 2048], P('llm', 'enc')
- grad_patches: bfloat16 [16384, 5120], P('enc', 'llm')
Inputs may be any that keep to these rules, and one draw needn't show every extreme that they name: Among the 128 consecutive tokens of one aligned block, no owner is named more than 2 times, a bound that some block reaches.
All inputs are finite; a program needn't handle non-finite values.
Results may differ from a plain program's by a relative error of at most 0.018.
Values may be sent and summed in bfloat16 or wider, within the bound.
No kernel may reach another device: no remote copies, remote signals or barrier semaphores. Data moves between devices by JAX's collectives and lax.ppermute only.
A program may use at most 192 MiB of HBM per device.

v0:
```python
import jax
import jax.numpy as jnp
from jax import lax
from jax.sharding import PartitionSpec as P

VD = 1280
MERGE = 4
EPSILON = 1e-06
HALF_ROOT = 0.7071067811865476
DENSITY = 0.3989422804014327


def cut_along(shard, dim, devices):
    before, after = (shard.shape[:dim], shard.shape[dim + 1 :])
    return jnp.moveaxis(shard.reshape(*before, devices, -1, *after), dim, 0)


def sent_and_summed(shard, axis, dim):
    devices = lax.axis_size(axis)
    pieces = lax.all_to_all(cut_along(shard, dim, devices), axis, 0, 0, tiled=True)
    return jnp.sum(pieces.astype(jnp.float32), axis=0)


def in_order(pieces, dim):
    dims = list(pieces.shape[1:])
    dims[dim] *= pieces.shape[0]
    return jnp.moveaxis(pieces, 0, dim).reshape(dims)


def copy_for_each(shard, axis):
    devices = lax.axis_size(axis)
    return lax.all_to_all(
        jnp.broadcast_to(shard[None], (devices, *shard.shape)), axis, 0, 0, tiled=True
    )


def collect(shard, axis, dim):
    return in_order(copy_for_each(shard, axis), dim)


def gelu_slope(hidden):
    cdf = 0.5 * (1.0 + lax.erf(hidden * HALF_ROOT))
    return cdf + hidden * jnp.exp(-0.5 * hidden * hidden) * DENSITY


def local(patches, ln_gain, w_in, b_in, w_out, b_out, owner, cotangent):
    group_size = lax.axis_size("llm")
    enc_size = lax.axis_size("enc")
    devices = enc_size * group_size
    slot_cap = cotangent.shape[0] // devices
    gathered = lax.all_gather(patches, "llm", axis=1, tiled=True)
    tokens = gathered.shape[0]
    merged = gathered.astype(jnp.float32).reshape(tokens, MERGE, VD)
    inverse = lax.rsqrt(jnp.mean(merged * merged, axis=-1, keepdims=True) + EPSILON)
    normed = (
        (merged * inverse * ln_gain.astype(jnp.float32))
        .reshape(tokens, MERGE * VD)
        .astype(jnp.bfloat16)
    )
    hidden = jnp.dot(normed, w_in, preferred_element_type=jnp.float32) + b_in.astype(jnp.float32)
    active = jax.nn.gelu(hidden, approximate=False).astype(jnp.bfloat16)
    own_rows = tokens // group_size
    summed = sent_and_summed(
        jnp.dot(active, w_out, preferred_element_type=jnp.float32).astype(jnp.bfloat16), "llm", 0
    )
    embeds = (summed + b_out.astype(jnp.float32)).astype(jnp.bfloat16)
    targets = owner[:, 0]
    before = jnp.arange(own_rows)[:, None] > jnp.arange(own_rows)[None, :]
    same_owner = targets[:, None] == targets[None, :]
    rank_in = jnp.sum(jnp.logical_and(same_owner, before), axis=1)
    slot_ids = targets * slot_cap + rank_in
    placing = (
        jnp.arange(devices * slot_cap, dtype=jnp.int32)[:, None] == slot_ids[None, :]
    ).astype(jnp.bfloat16)
    outgoing = jnp.dot(placing, embeds, preferred_element_type=jnp.float32).astype(jnp.bfloat16)
    image_embeds = lax.all_to_all(outgoing, ("enc", "llm"), split_axis=0, concat_axis=0, tiled=True)
    returned = lax.all_to_all(cotangent, ("enc", "llm"), split_axis=0, concat_axis=0, tiled=True)
    own_grad = jnp.dot(placing.T, returned, preferred_element_type=jnp.float32).astype(jnp.bfloat16)
    grad_embeds = collect(own_grad, "llm", 0)
    grad_active = lax.dot_general(
        grad_embeds, w_out, (((1,), (1,)), ((), ())), preferred_element_type=jnp.float32
    )
    grad_hidden = (grad_active * gelu_slope(hidden)).astype(jnp.bfloat16)
    out_term = lax.dot_general(
        active, grad_embeds, (((0,), (0,)), ((), ())), preferred_element_type=jnp.float32
    )
    grad_w_out = lax.psum_scatter(
        out_term.astype(jnp.bfloat16), "enc", scatter_dimension=1, tiled=True
    ).astype(jnp.float32)
    grad_w_in = lax.psum_scatter(
        lax.dot_general(
            normed, grad_hidden, (((0,), (0,)), ((), ())), preferred_element_type=jnp.float32
        ).astype(jnp.bfloat16),
        "enc",
        scatter_dimension=0,
        tiled=True,
    ).astype(jnp.float32)
    feature_term = lax.dot_general(
        grad_hidden, w_in, (((1,), (1,)), ((), ())), preferred_element_type=jnp.float32
    )
    grad_normed = sent_and_summed(feature_term.astype(jnp.bfloat16), "llm", 1)
    own_count = patches.shape[1] // VD
    local_inverse = lax.dynamic_slice_in_dim(
        inverse, lax.axis_index("llm") * own_count, own_count, 1
    )
    local_x = patches.astype(jnp.float32).reshape(tokens, own_count, VD)
    scaled = grad_normed.reshape(tokens, own_count, VD) * ln_gain.astype(jnp.float32)
    projection = jnp.mean(scaled * local_x, axis=-1, keepdims=True)
    cubed = local_inverse * local_inverse * local_inverse
    grad_patches = (
        (local_inverse * scaled - local_x * cubed * projection)
        .reshape(tokens, own_count * VD)
        .astype(jnp.bfloat16)
    )
    return (image_embeds, grad_w_in, grad_w_out, grad_patches)


def solution(mesh):
    in_specs = (
        P("enc", "llm"),
        P(),
        P(None, "llm"),
        P("llm"),
        P("llm", None),
        P(),
        P(("enc", "llm"), None),
        P(("enc", "llm"), None),
    )
    out_specs = (P(("enc", "llm"), None), P("enc", "llm"), P("llm", "enc"), P("enc", "llm"))
    return jax.shard_map(local, mesh=mesh, in_specs=in_specs, out_specs=out_specs, check_vma=False)
```

profile of v0, /device:TPU:0, one launch (start us, length us, event | category | flops | bytes accessed | tf_op | source)
XLA Modules:
  0.0 377.8 jit_solution(15109931664863186243)
XLA Ops:
  7.9 2.5 all_to_all.29
  10.5 11.2 %all-to-all-start.2 = ((bf16[128,2,2048]{2,1,0:T(2,128)(2,1)}), bf16[128,2,2048]{2,1,0:T(2,128)(2,1)S(1)}, u32[]{:S(2)}, u32[]{:S(2)}) async-start(bf16[128,2,2048]{2,1,0:T(2,128)(2,1)} %all_to_all.29), calls=%async_computation.2 | async-start | bytes 2097152 | tf_op jit(solution)/shard_map/all_to_all | solution.py:77
  21.9 18.4 %all-to-all-done.2 = bf16[128,2,2048]{2,1,0:T(2,128)(2,1)S(1)} async-done(((bf16[128,2,2048]{2,1,0:T(2,128)(2,1)}), bf16[128,2,2048]{2,1,0:T(2,128)(2,1)S(1)}, u32[]{:S(2)}, u32[]{:S(2)}) %all-to-all-start.2) | async-done | bytes 1048608 | tf_op jit(solution)/shard_map/all_to_all | solution.py:77
  41.1 1.6 broadcast_in_dim.2
  42.7 4.5 %all-to-all-start.3 = ((bf16[4,128,2048]{2,1,0:T(8,128)(2,1)}), bf16[4,128,2048]{2,1,0:T(8,128)(2,1)}, u32[]{:S(2)}, u32[]{:S(2)}) async-start(bf16[4,128,2048]{2,1,0:T(8,128)(2,1)} %broadcast_in_dim.2), calls=%async_computation.3 | async-start | bytes 4194304 | tf_op jit(solution)/shard_map/all_to_all | solution.py:32
  47.2 53.2 %all-gather.2.cloned.1.call-done = bf16[512,5120]{1,0:T(8,128)(2,1)} async-done(((bf16[512,1280]{1,0:T(8,128)(2,1)}), bf16[512,5120]{1,0:T(8,128)(2,1)}) %all-gather.2.cloned.1.call-update) | async-done | bytes 5242896 | tf_op jit(solution)/shard_map/all_gather | solution.py:51
  100.4 7.8 %convert_multiply_fusion.1 = f32[512,5120]{1,0:T(8,128)} fusion(bf16[512,5120]{1,0:T(8,128)(2,1)} %all-gather.2.cloned.1.call-done), kind=kLoop, calls=%fused_computation.2 | loop fusion | flops 5242880 | bytes 15728640 | tf_op jit(solution)/shard_map/mul | solution.py:54
  108.2 13.6 %mul.129 = f32[512,4,1280]{2,1,0:T(4,128)} reshape(f32[512,5120]{1,0:T(8,128)} %convert_multiply_fusion.1) | data formatting | bytes 20971520 | tf_op jit(solution)/shard_map/mul | solution.py:54
  121.8 5.4 %reduce_sum.46 = f32[512,4]{1,0:T(8,128)S(1)} reduce(f32[512,4,1280]{2,1,0:T(4,128)} %mul.129, f32[]{:T(128)} %constant.40.clone.1), dimensions={2}, to_apply=%region_1.0 | reduce | flops 2619392 | bytes 10493956 | tf_op jit(solution)/shard_map/reduce_sum | solution.py:54
  127.3 1.4 mul.130
  128.7 6.3 %copy.17 = f32[64,8,4,1280]{3,1,2,0:T(8,128)} copy(f32[64,8,4,1280]{3,2,1,0:T(4,128)S(1)} %bitcast.29) | data formatting | bytes 20971520
  135.0 9.6 %fusion.1 = bf16[512,5120]{1,0:T(8,128)(2,1)} fusion(f32[512,5120]{1,0:T(8,128)} %bitcast.28, bf16[512,5120]{1,0:T(8,128)(2,1)} %all-gather.2.cloned.1.call-done, f32[5120]{0:T(1024)S(1)} %mul.134), kind=kLoop, calls=%fused_computation.4 | loop fusion | flops 10485760 | bytes 20992000 | tf_op jit(solution)/shard_map/convert_element_type | solution.py:58
  144.6 19.1 %fusion.9 = (bf16[512,1280]{1,0:T(8,128)(2,1)S(1)}, f32[512,1280]{1,0:T(8,128)}) fusion(f32[1280]{0:T(1024)S(1)} %convert_element_type.69, bf16[512,5120]{1,0:T(8,128)(2,1)} %fusion.1, bf16[5120,1280]{1,0:T(8,128)(2,1)} %param.10), kind=kOutput, calls=%fused_computation.24 | convolution fusion | flops 6754140160 | bytes 22287360 | tf_op jit(solution)/shard_map/dot_general | solution.py:60
  163.7 6.8 %convolution_convert_fusion.1 = bf16[1280,2048]{0,1:T(8,128)(2,1)} fusion(bf16[512,1280]{1,0:T(8,128)(2,1)S(1)} %get-tuple-element.4, bf16[512,2048]{1,0:T(8,128)(2,1)} %bitcast.2), kind=kOutput, calls=%fused_computation.6 | convolution fusion | flops 2686976000 | bytes 8650752 | tf_op jit(solution)/shard_map/dot_general | solution.py:84
  170.8 7.5 %fusion.2 = bf16[512,1280]{1,0:T(8,128)(2,1)S(1)} fusion(bf16[512,2048]{1,0:T(8,128)(2,1)} %bitcast.2, bf16[1280,2048]{1,0:T(8,128)(2,1)} %param.12, f32[512,1280]{1,0:T(8,128)} %get-tuple-element.5), kind=kOutput, calls=%fused_computation.16 | convolution fusion | flops 2690908160 | bytes 11272192 | tf_op jit(solution)/shard_map/dot_general | solution.py:80
  178.3 1.0 copy-done.5
  179.4 10.0 %convolution_convert_fusion = bf16[5120,1280]{1,0:T(8,128)(2,1)} fusion(bf16[512,5120]{1,0:T(8,128)(2,1)S(1)} %bitcast.33, bf16[512,1280]{1,0:T(8,128)(2,1)S(1)} %fusion.2), kind=kOutput, calls=%fused_computation | convolution fusion | flops 6717440000 | bytes 19660800 | tf_op jit(solution)/shard_map/dot_general | solution.py:91
  189.4 6.7 %convolution_convert_fusion.3 = bf16[512,2048]{1,0:T(8,128)(2,1)} fusion(bf16[512,1280]{1,0:T(8,128)(2,1)S(1)} %get-tuple-element.4, bf16[1280,2048]{1,0:T(8,128)(2,1)} %param.12), kind=kOutput, calls=%fused_computation.17 | convolution fusion | flops 2685403136 | bytes 8650752 | tf_op jit(solution)/shard_map/dot_general | solution.py:64
  196.2 3.8 all-to-all-start
  200.0 26.7 %all-to-all-done = bf16[4,128,2048]{2,1,0:T(8,128)(2,1)S(1)} async-done(((bf16[4,128,2048]{2,1,0:T(8,128)(2,1)}), bf16[4,128,2048]{2,1,0:T(8,128)(2,1)S(1)}, u32[]{:S(2)}, u32[]{:S(2)}) %all-to-all-start) | async-done | bytes 2097184 | tf_op jit(solution)/shard_map/all_to_all | solution.py:20
  227.5 1.5 all_to_all.26
  229.0 8.7 %all-to-all-start.1 = ((bf16[128,2,2048]{2,1,0:T(2,128)(2,1)}), bf16[128,2,2048]{2,1,0:T(2,128)(2,1)S(1)}, u32[]{:S(2)}, u32[]{:S(2)}) async-start(bf16[128,2,2048]{2,1,0:T(2,128)(2,1)} %all_to_all.26), calls=%async_computation.1 | async-start | bytes 2097152 | tf_op jit(solution)/shard_map/all_to_all | solution.py:76
  237.8 13.5 %convolution_convert_fusion.2 = bf16[512,5120]{1,0:T(8,128)(2,1)} fusion(bf16[512,1280]{1,0:T(8,128)(2,1)S(1)} %copy-done.6, bf16[5120,1280]{1,0:T(8,128)(2,1)} %param.10), kind=kOutput, calls=%fused_computation.7 | convolution fusion | flops 6713507840 | bytes 19660800 | tf_op jit(solution)/shard_map/dot_general | solution.py:98
  251.2 5.1 %copy.19 = bf16[64,4,8,1280]{3,2,0,1:T(8,128)(2,1)} copy(bf16[64,4,8,1280]{3,2,1,0:T(8,128)(2,1)} %bitcast.31) | data formatting | bytes 10485760 | tf_op jit(solution)/shard_map/reshape | solution.py:15
  257.2 5.2 %all-to-all-start.4 = ((bf16[4,512,1280]{2,1,0:T(8,128)(2,1)}), bf16[4,512,1280]{2,1,0:T(8,128)(2,1)}, u32[]{:S(2)}, u32[]{:S(2)}) async-start(bf16[4,512,1280]{2,1,0:T(8,128)(2,1)} %bitcast.30), calls=%async_computation.6 | async-start | bytes 10485760 | tf_op jit(solution)/shard_map/all_to_all | solution.py:20
  262.6 1.2 all_to_all.28
  263.8 59.2 %all-to-all-done.4 = bf16[4,512,1280]{2,1,0:T(8,128)(2,1)} async-done(((bf16[4,512,1280]{2,1,0:T(8,128)(2,1)}), bf16[4,512,1280]{2,1,0:T(8,128)(2,1)}, u32[]{:S(2)}, u32[]{:S(2)}) %all-to-all-start.4) | async-done | bytes 5242912 | tf_op jit(solution)/shard_map/all_to_all | solution.py:20
  323.0 3.7 convert_reduce_fusion
  327.1 1.7 fusion.5
  328.8 1.7 convert_element_type.81
  330.5 38.8 %reduce-scatter.3.cloned.1.call-done = bf16[160,1280]{1,0:T(8,128)(2,1)} async-done(((bf16[5120,1280]{1,0:T(8,128)(2,1)}), bf16[160,1280]{1,0:T(8,128)(2,1)}) %reduce-scatter.3.cloned.1.call-update) | async-done | bytes 409616 | tf_op jit(solution)/shard_map/reduce_scatter | solution.py:90
  369.3 1.9 convert_element_type.79
  (43 shorter events, 4.4 us)
Async XLA Ops:
  7.2 14.5 %copy-start.1 = (bf16[1280]{0:T(1024)(128)(2,1)S(1)}, bf16[1280]{0:T(1024)(128)(2,1)}, u32[]{:S(2)}) copy-start(bf16[1280]{0:T(1024)(128)(2,1)} %param.9) | copy-start | bytes 7684
  7.2 14.5 %copy-start.2 = (bf16[1280]{0:T(1024)(128)(2,1)S(1)}, bf16[1280]{0:T(1024)(128)(2,1)}, u32[]{:S(2)}) copy-start(bf16[1280]{0:T(1024)(128)(2,1)} %param.11) | copy-start | bytes 7684
  7.2 14.5 %copy-start.4 = (s32[128,1]{0,1:T(1,128)S(1)}, s32[128,1]{0,1:T(1,128)}, u32[]{:S(2)}) copy-start(s32[128,1]{0,1:T(1,128)} %param.14) | copy-start | bytes 1540
  7.2 93.2 %all-gather.2.cloned.1.call-start = ((), (), s32[]{:S(2)}) async-start(), calls=%async_computation.7 | async-start | bytes 6553600 | tf_op jit(solution)/shard_map/all_gather | solution.py:51
  10.5 29.8 %all-to-all-start.2 = ((bf16[128,2,2048]{2,1,0:T(2,128)(2,1)}), bf16[128,2,2048]{2,1,0:T(2,128)(2,1)S(1)}, u32[]{:S(2)}, u32[]{:S(2)}) async-start(bf16[128,2,2048]{2,1,0:T(2,128)(2,1)} %all_to_all.29), calls=%async_computation.2 | async-start | bytes 2097152 | tf_op jit(solution)/shard_map/all_to_all | solution.py:77
  42.7 121.0 %all-to-all-start.3 = ((bf16[4,128,2048]{2,1,0:T(8,128)(2,1)}), bf16[4,128,2048]{2,1,0:T(8,128)(2,1)}, u32[]{:S(2)}, u32[]{:S(2)}) async-start(bf16[4,128,2048]{2,1,0:T(8,128)(2,1)} %broadcast_in_dim.2), calls=%async_computation.3 | async-start | bytes 4194304 | tf_op jit(solution)/shard_map/all_to_all | solution.py:32
  47.2 281.7 %reduce-scatter.5.cloned.1.call-start = ((), (), s32[]{:S(2)}) async-start(), calls=%async_computation.9 | async-start | bytes 5406720 | tf_op jit(solution)/shard_map/reduce_scatter | solution.py:87
  170.5 8.9 %slice-start = ((s8[5242880]{0:T(1024)(128)(4,1)}), s8[1048576]{0:T(1024)(128)(4,1)S(1)}, s32[]{:S(2)}) async-start(s8[5242880]{0:T(1024)(128)(4,1)} %bitcast.32), calls=%async_computation.10 | async-start | bytes 2097152
  170.5 198.8 %reduce-scatter.3.cloned.1.call-start = ((), (), s32[]{:S(2)}) async-start(), calls=%async_computation.8 | async-start | bytes 13516800 | tf_op jit(solution)/shard_map/reduce_scatter | solution.py:90
  170.8 8.6 %slice-start.1 = ((s8[5242880]{0:T(1024)(128)(4,1)}), s8[4194304]{0:T(1024)(128)(4,1)S(1)}, s32[]{:S(2)}) async-start(s8[5242880]{0:T(1024)(128)(4,1)} %bitcast.32), calls=%async_computation.11 | async-start | bytes 8388608
  178.3 1.1 copy-start.5
  196.2 3.8 copy-start.3
  196.2 30.5 %all-to-all-start = ((bf16[4,128,2048]{2,1,0:T(8,128)(2,1)}), bf16[4,128,2048]{2,1,0:T(8,128)(2,1)S(1)}, u32[]{:S(2)}, u32[]{:S(2)}) async-start(bf16[4,128,2048]{2,1,0:T(8,128)(2,1)} %bitcast.34), calls=%async_computation | async-start | bytes 4194304 | tf_op jit(solution)/shard_map/all_to_all | solution.py:20
  227.5 10.2 %copy-start.6 = (bf16[512,1280]{1,0:T(8,128)(2,1)S(1)}, bf16[512,1280]{1,0:T(8,128)(2,1)}, u32[]{:S(2)}) copy-start(bf16[512,1280]{1,0:T(8,128)(2,1)} %copy-done.5) | copy-start | bytes 3932164
  229.0 28.1 %all-to-all-start.1 = ((bf16[128,2,2048]{2,1,0:T(2,128)(2,1)}), bf16[128,2,2048]{2,1,0:T(2,128)(2,1)S(1)}, u32[]{:S(2)}, u32[]{:S(2)}) async-start(bf16[128,2,2048]{2,1,0:T(2,128)(2,1)} %all_to_all.26), calls=%async_computation.1 | async-start | bytes 2097152 | tf_op jit(solution)/shard_map/all_to_all | solution.py:76
  257.2 65.8 %all-to-all-start.4 = ((bf16[4,512,1280]{2,1,0:T(8,128)(2,1)}), bf16[4,512,1280]{2,1,0:T(8,128)(2,1)}, u32[]{:S(2)}, u32[]{:S(2)}) async-start(bf16[4,512,1280]{2,1,0:T(8,128)(2,1)} %bitcast.30), calls=%async_computation.6 | async-start | bytes 10485760 | tf_op jit(solution)/shard_map/all_to_all | solution.py:20
  263.8 62.9 %copy-start = (bf16[512,1280]{1,0:T(8,128)(2,1)S(1)}, bf16[512,1280]{1,0:T(8,128)(2,1)}, u32[]{:S(2)}) copy-start(bf16[512,1280]{1,0:T(8,128)(2,1)} %param.8) | copy-start | bytes 3932164
Sparse Core Ops, SparseCore 0:
  9.7 90.7 all-gather.1
  170.6 90.3 reduce-scatter.4
  264.9 104.3 reduce-scatter.2
where the time goes:
time: 379 us; the launch traced here: 378 us
  waiting for transfers between devices  198 us (52%)
  matrix products  64.4 us (17%)
  local copies, waits for them, and re-layouts  35 us (9%)
  starting transfers between devices  33.6 us (9%)
  other arithmetic  32.9 us (9%)
  between operations  14 us (4%)
    all_to_all x2, waiting for transfers between devices, sent_and_summed(): lax.all_to_all(cut_along(shard, dim, devices), axis, 0, 0, tiled=True)  85.9 us
    all_gather x1, waiting for transfers between devices, local(): gathered = lax.all_gather(patches, 'llm', axis=1, tiled=True)  53.2 us
    reduce_scatter x1, waiting for transfers between devices, local(): lax.psum_scatter(lax.dot_general(normed, grad_hidden, (((0,), (0,)), ((),...  38.8 us
    dot_general x1, matrix products, local(): jnp.dot(normed, w_in, preferred_element_type=jnp.float32)  19.1 us
    all_to_all x1, waiting for transfers between devices, local(): lax.all_to_all(cotangent, ('enc', 'llm'), split_axis=0, concat_axis=0, ti...  18.4 us
    mul x1, local copies, waits for them, and re-layouts, local(): merged * merged  13.6 us
    dot_general x1, matrix products, local(): lax.dot_general(grad_hidden, w_in, (((1,), (1,)), ((), ())), preferred_el...  13.5 us
    all_to_all x1, starting transfers between devices, local(): lax.all_to_all(cotangent, ('enc', 'llm'), split_axis=0, concat_axis=0, ti...  11.2 us
  transfers between devices with their start and end apart: 8, of which 6 were waited for; matrix products, arithmetic and copies ran while one was open for 31% of the time, Pallas kernels for 0%

commit v1 on v0

--- a/solution.py
+++ b/solution.py
@@ -48,7 +48,11 @@
     enc_size = lax.axis_size("enc")
     devices = enc_size * group_size
     slot_cap = cotangent.shape[0] // devices
-    gathered = lax.all_gather(patches, "llm", axis=1, tiled=True)
+    dev_n = lax.axis_size("llm")
+    block_now = tuple((dev_n if q == 1 else 1 for q in range(patches.ndim)))
+    gathered = lax.all_to_all(
+        jnp.tile(patches, block_now), "llm", split_axis=1, concat_axis=1, tiled=True
+    )
     tokens = gathered.shape[0]
     merged = gathered.astype(jnp.float32).reshape(tokens, MERGE, VD)
     inverse = lax.rsqrt(jnp.mean(merged * merged, axis=-1, keepdims=True) + EPSILON)

time: 379 us -> 358 us (0.945)
  blocking collectives: 0 us -> 29.6 us
  other arithmetic: 32.9 us -> 14.9 us
  waiting for transfers between devices: 198 us -> 184 us
  starting transfers between devices: 33.6 us -> 23.9 us
  local copies, waits for them, and re-layouts: 35 us -> 27.4 us
    all_gather x1 -> x0, waiting for transfers between devices: 53.2 us -> none  [local(): gathered = lax.all_gather(patches, 'llm', axis=1, tiled=True)]
    all_to_all x1, waiting for transfers between devices: 18.4 us -> 59.6 us  [local(): lax.all_to_all(jnp.tile(patches, block_now), 'llm', split_axis=1, concat_...]
    all_to_all x0 -> x1, blocking collectives: none -> 29.6 us  [local(): lax.all_to_all(cotangent, ('enc', 'llm'), split_axis=0, concat_axis=0, ti...]
    mul x4 -> x0, local copies, waits for them, and re-layouts: 15 us -> none  [the longest x1 13.6 us: local(): merged * merged]
    convert_element_type x1, other arithmetic: 9.63 us -> 1.23 us  [local(): normed = (merged * inverse * ln_gain.astype(jnp.float32)).reshape(tokens,...]
    all_to_all x0 -> x1, local copies, waits for them, and re-layouts: none -> 7.89 us  [local(): lax.all_to_all(jnp.tile(patches, block_now), 'llm', split_axis=1, concat_...]
    mul x1 -> x0, other arithmetic: 7.78 us -> none  [local(): merged * merged]
    all_to_all x1, starting transfers between devices: 11.2 us -> 5.2 us  [local(): lax.all_to_all(jnp.tile(patches, block_now), 'llm', split_axis=1, concat_...]
  transfers between devices with their start and end apart: 8 -> 7, of which waited for: 6 -> 5; matrix products, arithmetic and copies ran while one was open for 31% -> 23% of each run, Pallas kernels for 0% -> 0%
where the time goes in v1:
time: 358 us; the launch traced here: 357 us
  waiting for transfers between devices  184 us (51%)
  matrix products  63.3 us (18%)
  blocking collectives  29.6 us (8%)
  local copies, waits for them, and re-layouts  27.4 us (8%)
  starting transfers between devices  23.9 us (7%)
  other arithmetic  14.9 us (4%)
  between operations  14.2 us (4%)
    all_to_all x2, waiting for transfers between devices, sent_and_summed(): lax.all_to_all(cut_along(shard, dim, devices), axis, 0, 0, tiled=True)  84.9 us
    all_to_all x1, waiting for transfers between devices, local(): lax.all_to_all(jnp.tile(patches, block_now), 'llm', split_axis=1, concat_...  59.6 us
    reduce_scatter x1, waiting for transfers between devices, local(): lax.psum_scatter(lax.dot_general(normed, grad_hidden, (((0,), (0,)), ((),...  38.8 us
    all_to_all x1, blocking collectives, local(): lax.all_to_all(cotangent, ('enc', 'llm'), split_axis=0, concat_axis=0, ti...  29.6 us
    dot_general x1, matrix products, local(): jnp.dot(normed, w_in, preferred_element_type=jnp.float32)  18 us
    dot_general x1, matrix products, local(): lax.dot_general(grad_hidden, w_in, (((1,), (1,)), ((), ())), preferred_el...  13.7 us
    dot_general x1, matrix products, local(): lax.dot_general(normed, grad_hidden, (((0,), (0,)), ((), ())), preferred_...  9.89 us
    all_to_all x2, starting transfers between devices, sent_and_summed(): lax.all_to_all(cut_along(shard, dim, devices), axis, 0, 0, tiled=True)  9.7 us
  transfers between devices with their start and end apart: 7, of which 5 were waited for; matrix products, arithmetic and copies ran while one was open for 23% of the time, Pallas kernels for 0%

profile of v1, /device:TPU:0, one launch (start us, length us, event | category | flops | bytes accessed | tf_op | source)
XLA Modules:
  0.0 357.3 jit_solution(6705087031440137952)
XLA Ops:
  7.2 1.9 all_to_all.34
  9.0 29.6 %all_to_all.45 = bf16[128,2,2048]{2,1,0:T(2,128)(2,1)S(1)} all-to-all(bf16[128,2,2048]{2,1,0:T(2,128)(2,1)S(1)} %all_to_all.34), channel_id=1, replica_groups=mesh['enc'=32,'llm'=4] {'enc','llm'}, dimensions={0} | all-to-all | bytes 2097152 | tf_op jit(solution)/shard_map/all_to_all | solution.py:81
  38.6 2.7 tile.2
  41.3 5.2 %all-to-all-start = ((bf16[512,4,1280]{2,0,1:T(8,128)(2,1)}), bf16[512,4,1280]{2,0,1:T(8,128)(2,1)}, u32[]{:S(2)}, u32[]{:S(2)}) async-start(bf16[512,4,1280]{2,0,1:T(8,128)(2,1)} %tile.2), calls=%async_computation | async-start | bytes 10485760 | tf_op jit(solution)/shard_map/all_to_all | solution.py:53
  47.6 59.6 %all-to-all-done = bf16[512,4,1280]{2,0,1:T(8,128)(2,1)} async-done(((bf16[512,4,1280]{2,0,1:T(8,128)(2,1)}), bf16[512,4,1280]{2,0,1:T(8,128)(2,1)}, u32[]{:S(2)}, u32[]{:S(2)}) %all-to-all-start) | async-done | bytes 5242912 | tf_op jit(solution)/shard_map/all_to_all | solution.py:53
  107.2 1.6 broadcast_in_dim.2
  108.8 3.6 %all-to-all-start.4 = ((bf16[4,128,2048]{2,1,0:T(8,128)(2,1)}), bf16[4,128,2048]{2,1,0:T(8,128)(2,1)S(1)}, u32[]{:S(2)}, u32[]{:S(2)}) async-start(bf16[4,128,2048]{2,1,0:T(8,128)(2,1)} %broadcast_in_dim.2), calls=%async_computation.4 | async-start | bytes 4194304 | tf_op jit(solution)/shard_map/all_to_all | solution.py:32
  112.6 7.9 %copy.16 = bf16[512,4,1280]{0,2,1:T(8,128)(2,1)} copy(bf16[512,4,1280]{2,0,1:T(8,128)(2,1)} %all-to-all-done) | data formatting | bytes 10485760 | tf_op jit(solution)/shard_map/all_to_all | solution.py:53
  120.5 3.7 %fusion = f32[512,4]{0,1:T(4,128)S(1)} fusion(bf16[512,4,1280]{0,2,1:T(8,128)(2,1)} %copy.16), kind=kLoop, calls=%fused_computation.3 | loop fusion | flops 7862272 | bytes 5251072 | tf_op jit(solution)/shard_map/reduce_sum | solution.py:58
  124.6 1.2 fusion.2
  125.8 2.3 copy-done.2
  128.1 18.0 %fusion.10 = (bf16[512,1280]{1,0:T(8,128)(2,1)}, f32[512,1280]{1,0:T(8,128)}) fusion(f32[1280]{0:T(1024)S(1)} %convert_element_type.74, bf16[512,5120]{0,1:T(8,128)(2,1)S(1)} %bitcast.30, bf16[5120,1280]{1,0:T(8,128)(2,1)} %param.10), kind=kOutput, calls=%fused_computation.25 | convolution fusion | flops 6754140160 | bytes 22287360 | tf_op jit(solution)/shard_map/dot_general | solution.py:64
  146.1 6.7 %convolution_convert_fusion.1 = bf16[1280,2048]{0,1:T(8,128)(2,1)} fusion(bf16[512,1280]{1,0:T(8,128)(2,1)} %get-tuple-element.6, bf16[512,2048]{1,0:T(8,128)(2,1)S(1)} %bitcast.35), kind=kOutput, calls=%fused_computation.7 | convolution fusion | flops 2686976000 | bytes 8650752 | tf_op jit(solution)/shard_map/dot_general | solution.py:88
  153.2 7.5 %fusion.3 = bf16[512,1280]{1,0:T(8,128)(2,1)S(1)} fusion(bf16[512,2048]{1,0:T(8,128)(2,1)} %bitcast.36, bf16[1280,2048]{1,0:T(8,128)(2,1)} %param.12, f32[512,1280]{1,0:T(8,128)} %get-tuple-element.7), kind=kOutput, calls=%fused_computation.17 | convolution fusion | flops 2690908160 | bytes 11272192 | tf_op jit(solution)/shard_map/dot_general | solution.py:84
  160.7 1.1 copy-done.9
  161.7 9.9 %convolution_convert_fusion = bf16[5120,1280]{1,0:T(8,128)(2,1)} fusion(bf16[512,5120]{0,1:T(8,128)(2,1)S(1)} %bitcast.33, bf16[512,1280]{1,0:T(8,128)(2,1)S(1)} %fusion.3), kind=kOutput, calls=%fused_computation | convolution fusion | flops 6717440000 | bytes 19660800 | tf_op jit(solution)/shard_map/dot_general | solution.py:95
  171.7 1.3 copy-done.8
  173.0 6.7 %convolution_convert_fusion.3 = bf16[512,2048]{1,0:T(8,128)(2,1)} fusion(bf16[512,1280]{1,0:T(8,128)(2,1)S(1)} %copy-done.8, bf16[1280,2048]{1,0:T(8,128)(2,1)} %param.12), kind=kOutput, calls=%fused_computation.18 | convolution fusion | flops 2685403136 | bytes 8650752 | tf_op jit(solution)/shard_map/dot_general | solution.py:68
  179.7 4.6 %all-to-all-start.1 = ((bf16[4,128,2048]{2,1,0:T(8,128)(2,1)}), bf16[4,128,2048]{2,1,0:T(8,128)(2,1)S(1)}, u32[]{:S(2)}, u32[]{:S(2)}) async-start(bf16[4,128,2048]{2,1,0:T(8,128)(2,1)} %bitcast.37), calls=%async_computation.1 | async-start | bytes 4194304 | tf_op jit(solution)/shard_map/all_to_all | solution.py:20
  184.4 25.5 %all-to-all-done.1 = bf16[4,128,2048]{2,1,0:T(8,128)(2,1)S(1)} async-done(((bf16[4,128,2048]{2,1,0:T(8,128)(2,1)}), bf16[4,128,2048]{2,1,0:T(8,128)(2,1)S(1)}, u32[]{:S(2)}, u32[]{:S(2)}) %all-to-all-start.1) | async-done | bytes 2097184 | tf_op jit(solution)/shard_map/all_to_all | solution.py:20
  210.7 1.5 all_to_all.31
  212.2 4.9 %all-to-all-start.2 = ((bf16[128,2,2048]{2,1,0:T(2,128)(2,1)}), bf16[128,2,2048]{2,1,0:T(2,128)(2,1)S(1)}, u32[]{:S(2)}, u32[]{:S(2)}) async-start(bf16[128,2,2048]{2,1,0:T(2,128)(2,1)} %all_to_all.31), calls=%async_computation.2 | async-start | bytes 2097152 | tf_op jit(solution)/shard_map/all_to_all | solution.py:80
  217.1 13.7 %convolution_convert_fusion.2 = bf16[512,5120]{1,0:T(8,128)(2,1)} fusion(bf16[512,1280]{1,0:T(8,128)(2,1)} %copy-done.9, bf16[5120,1280]{1,0:T(8,128)(2,1)} %param.10), kind=kOutput, calls=%fused_computation.8 | convolution fusion | flops 6713507840 | bytes 19660800 | tf_op jit(solution)/shard_map/dot_general | solution.py:102
  230.7 5.1 %copy.20 = bf16[64,4,8,1280]{3,2,0,1:T(8,128)(2,1)} copy(bf16[64,4,8,1280]{3,2,1,0:T(8,128)(2,1)} %bitcast.34) | data formatting | bytes 10485760 | tf_op jit(solution)/shard_map/reshape | solution.py:15
  236.4 5.1 %all-to-all-start.5 = ((bf16[4,512,1280]{2,1,0:T(8,128)(2,1)}), bf16[4,512,1280]{2,1,0:T(8,128)(2,1)}, u32[]{:S(2)}, u32[]{:S(2)}) async-start(bf16[4,512,1280]{2,1,0:T(8,128)(2,1)} %bitcast.29), calls=%async_computation.7 | async-start | bytes 10485760 | tf_op jit(solution)/shard_map/all_to_all | solution.py:20
  241.5 1.2 all_to_all.33
  242.7 59.5 %all-to-all-done.5 = bf16[4,512,1280]{2,1,0:T(8,128)(2,1)} async-done(((bf16[4,512,1280]{2,1,0:T(8,128)(2,1)}), bf16[4,512,1280]{2,1,0:T(8,128)(2,1)}, u32[]{:S(2)}, u32[]{:S(2)}) %all-to-all-start.5) | async-done | bytes 5242912 | tf_op jit(solution)/shard_map/all_to_all | solution.py:20
  302.2 3.7 %convert_reduce_fusion = f32[512,1280]{1,0:T(8,128)S(1)} fusion(bf16[4,512,1280]{2,1,0:T(8,128)(2,1)} %all-to-all-done.5), kind=kLoop, calls=%fused_computation.6 | loop fusion | flops 4587520 | bytes 7864320 | tf_op jit(solution)/shard_map/reduce_sum | solution.py:21
  306.4 1.7 fusion.6
  308.0 1.7 convert_element_type.86
  309.7 38.8 %reduce-scatter.3.cloned.1.call-done = bf16[160,1280]{1,0:T(8,128)(2,1)} async-done(((bf16[5120,1280]{1,0:T(8,128)(2,1)}), bf16[160,1280]{1,0:T(8,128)(2,1)}) %reduce-scatter.3.cloned.1.call-update) | async-done | bytes 409616 | tf_op jit(solution)/shard_map/reduce_scatter | solution.py:94
  348.6 1.9 convert_element_type.84
  (42 shorter events, 3.7 us)
Async XLA Ops:
  7.2 31.5 %copy-start.1 = (bf16[512,1280]{1,0:T(8,128)(2,1)S(1)}, bf16[512,1280]{1,0:T(8,128)(2,1)}, u32[]{:S(2)}) copy-start(bf16[512,1280]{1,0:T(8,128)(2,1)} %param.8) | copy-start | bytes 3932164
  41.3 5.2 %copy-start.4 = (bf16[1280]{0:T(1024)(128)(2,1)S(1)}, bf16[1280]{0:T(1024)(128)(2,1)}, u32[]{:S(2)}) copy-start(bf16[1280]{0:T(1024)(128)(2,1)} %param.9) | copy-start | bytes 7684
  41.3 5.2 %copy-start.5 = (bf16[1280]{0:T(1024)(128)(2,1)S(1)}, bf16[1280]{0:T(1024)(128)(2,1)}, u32[]{:S(2)}) copy-start(bf16[1280]{0:T(1024)(128)(2,1)} %param.11) | copy-start | bytes 7684
  41.3 5.3 %copy-start.7 = (s32[128,1]{0,1:T(1,128)S(1)}, s32[128,1]{0,1:T(1,128)}, u32[]{:S(2)}) copy-start(s32[128,1]{0,1:T(1,128)} %param.14) | copy-start | bytes 1540
  41.3 65.9 %all-to-all-start = ((bf16[512,4,1280]{2,0,1:T(8,128)(2,1)}), bf16[512,4,1280]{2,0,1:T(8,128)(2,1)}, u32[]{:S(2)}, u32[]{:S(2)}) async-start(bf16[512,4,1280]{2,0,1:T(8,128)(2,1)} %tile.2), calls=%async_computation | async-start | bytes 10485760 | tf_op jit(solution)/shard_map/all_to_all | solution.py:53
  108.8 37.3 %all-to-all-start.4 = ((bf16[4,128,2048]{2,1,0:T(8,128)(2,1)}), bf16[4,128,2048]{2,1,0:T(8,128)(2,1)S(1)}, u32[]{:S(2)}, u32[]{:S(2)}) async-start(bf16[4,128,2048]{2,1,0:T(8,128)(2,1)} %broadcast_in_dim.2), calls=%async_computation.4 | async-start | bytes 4194304 | tf_op jit(solution)/shard_map/all_to_all | solution.py:32
  112.4 195.6 %reduce-scatter.5.cloned.1.call-start = ((), (), s32[]{:S(2)}) async-start(), calls=%async_computation.9 | async-start | bytes 5406720 | tf_op jit(solution)/shard_map/reduce_scatter | solution.py:91
  120.5 4.0 %copy-start = (bf16[512,4,1280]{0,2,1:T(8,128)(2,1)S(1)}, bf16[512,4,1280]{0,2,1:T(8,128)(2,1)}, u32[]{:S(2)}) copy-start(bf16[512,4,1280]{0,2,1:T(8,128)(2,1)} %copy.16) | copy-start | bytes 15728644
  125.8 2.3 copy-start.2
  146.1 6.7 %copy-start.3 = (bf16[4,128,2048]{2,1,0:T(8,128)(2,1)}, bf16[4,128,2048]{2,1,0:T(8,128)(2,1)S(1)}, u32[]{:S(2)}) copy-start(bf16[4,128,2048]{2,1,0:T(8,128)(2,1)S(1)} %all-to-all-done.4) | copy-start | bytes 6291460
  152.8 8.9 %slice-start = ((s8[5242880]{0:T(1024)(128)(4,1)}), s8[1048576]{0:T(1024)(128)(4,1)S(1)}, s32[]{:S(2)}) async-start(s8[5242880]{0:T(1024)(128)(4,1)} %bitcast.31), calls=%async_computation.10 | async-start | bytes 2097152
  152.9 195.7 %reduce-scatter.3.cloned.1.call-start = ((), (), s32[]{:S(2)}) async-start(), calls=%async_computation.8 | async-start | bytes 13516800 | tf_op jit(solution)/shard_map/reduce_scatter | solution.py:94
  153.1 8.6 %slice-start.1 = ((s8[5242880]{0:T(1024)(128)(4,1)}), s8[4194304]{0:T(1024)(128)(4,1)S(1)}, s32[]{:S(2)}) async-start(s8[5242880]{0:T(1024)(128)(4,1)} %bitcast.31), calls=%async_computation.11 | async-start | bytes 8388608
  160.7 1.1 copy-start.9
  171.6 1.4 copy-start.8
  179.7 4.7 %copy-start.6 = (bf16[2048]{0:T(1024)(128)(2,1)S(1)}, bf16[2048]{0:T(1024)(128)(2,1)}, u32[]{:S(2)}) copy-start(bf16[2048]{0:T(1024)(128)(2,1)} %param.13) | copy-start | bytes 12292
  179.7 30.1 %all-to-all-start.1 = ((bf16[4,128,2048]{2,1,0:T(8,128)(2,1)}), bf16[4,128,2048]{2,1,0:T(8,128)(2,1)S(1)}, u32[]{:S(2)}, u32[]{:S(2)}) async-start(bf16[4,128,2048]{2,1,0:T(8,128)(2,1)} %bitcast.37), calls=%async_computation.1 | async-start | bytes 4194304 | tf_op jit(solution)/shard_map/all_to_all | solution.py:20
  212.2 24.3 %all-to-all-start.2 = ((bf16[128,2,2048]{2,1,0:T(2,128)(2,1)}), bf16[128,2,2048]{2,1,0:T(2,128)(2,1)S(1)}, u32[]{:S(2)}, u32[]{:S(2)}) async-start(bf16[128,2,2048]{2,1,0:T(2,128)(2,1)} %all_to_all.31), calls=%async_computation.2 | async-start | bytes 2097152 | tf_op jit(solution)/shard_map/all_to_all | solution.py:80
  236.4 65.8 %all-to-all-start.5 = ((bf16[4,512,1280]{2,1,0:T(8,128)(2,1)}), bf16[4,512,1280]{2,1,0:T(8,128)(2,1)}, u32[]{:S(2)}, u32[]{:S(2)}) async-start(bf16[4,512,1280]{2,1,0:T(8,128)(2,1)} %bitcast.29), calls=%async_computation.7 | async-start | bytes 10485760 | tf_op jit(solution)/shard_map/all_to_all | solution.py:20
Sparse Core Ops, SparseCore 0:
  153.0 87.3 reduce-scatter.4
  244.3 104.2 reduce-scatter.2
